TPU v7x, 128 devices: a whole 4x4x4 slice. The times are simulated.
128 devices in a mesh: utt: 8 (over y, core), clu: 16 (over z, x).
Axes of the slice: x: 4, y: 4, z: 4, core: 2. Of those that a mesh axis runs over, the one named last changes fastest.
Arguments:
- features: bfloat16 [262144, 1280], P(('utt', 'clu')), may hold values from -1.75 to 1.75
- centroids: bfloat16 [2048, 1280], P('clu'), may hold values from -2 to 2
- route: int32 [128, 128], P(('utt', 'clu')), may hold values from 0 to 127, each once within a row
Outputs:
- trainer_labels: int32 [128, 128, 16], P(('utt', 'clu'))
- trainer_distance: float32 [128, 128, 16], P(('utt', 'clu'))
Inputs may be any that keep to these rules, and one draw needn't show every extreme that they name: Each row of route names every trainer device exactly once.
All inputs are finite; a program needn't handle non-finite values.
Results may differ from a plain program's by a relative error of at most 0.0003.
Values may be sent and summed in bfloat16 or wider, within the bound.
No kernel may reach another device: no remote copies, remote signals or barrier semaphores. Data moves between devices by JAX's collectives and lax.ppermute only.
A program may use at most 64 MiB of HBM per device.

v0:
```python
import functools

import jax
import jax.numpy as jnp
from jax import lax
from jax.experimental import pallas as pl
from jax.experimental.pallas import tpu as pltpu
from jax.sharding import PartitionSpec as P


AXES = ("utt", "clu")
SIDE = 4
OFFSETS = (0, 1, -1, 2)
VMEM = pltpu.VMEM
F32 = jnp.float32
BF16 = jnp.bfloat16
BIG = 1 << 20


def device(y, c, z, x):
    return (y * 2 + c) * 16 + (z % SIDE) * SIDE + x % SIDE


def along(offset, phase):
    pairs = []
    for y in range(4):
        for c in range(2):
            for z in range(SIDE):
                for x in range(SIDE):
                    on_x = (c == 0) == (phase == 0)
                    target = device(y, c, z, x + offset) if on_x else device(y, c, z + offset, x)
                    pairs.append((device(y, c, z, x), target))
    return pairs


def core_swap():
    return [
        (device(y, c, z, x), device(y, 1 - c, z, x))
        for y in range(4)
        for c in range(2)
        for z in range(SIDE)
        for x in range(SIDE)
    ]


def fetch(step):
    pairs = []
    for y in range(4):
        for c in range(2):
            for z in range(SIDE):
                for x in range(SIDE):
                    near = y % 2 + 2 * step
                    target = device(y, c, z - 2, x - near) if c == 0 else device(y, c, z - near, x - 2)
                    pairs.append((device(y, c, z, x), target))
    return pairs


def plane_swap():
    return [
        (device(y, c, z, x), device(y ^ 1, c, z, x))
        for y in range(4)
        for c in range(2)
        for z in range(SIDE)
        for x in range(SIDE)
    ]


def block_base(far, near, rows):
    core = lax.rem(lax.axis_index("utt"), 2)
    clu = lax.axis_index("clu")
    z, x = clu // SIDE, lax.rem(clu, SIDE)
    from_z = lax.rem(z + jnp.where(core == 0, far, near), SIDE)
    from_x = lax.rem(x + jnp.where(core == 0, near, far), SIDE)
    return (from_z * SIDE + from_x) * (2 * rows) + core * rows


def row_bases(far, rows):
    return [block_base((SIDE - far) % SIDE, (SIDE - near) % SIDE, rows) for near in OFFSETS]


def pair_bases(own, rows):
    plane = lax.rem(lax.axis_index("utt") // 2, 2)
    first = plane if own else 1 - plane
    return [block_base(2, lax.rem(first + 2 * step, SIDE), rows) for step in range(2)]


def cut_kernel(cents_ref, out_ref):
    rows = out_ref.shape[0]
    core = lax.rem(lax.axis_index("utt"), 2)
    out_ref[...] = cents_ref[pl.ds(pl.multiple_of(core * rows, rows), rows), :]


def cut(centroids):
    rows, width = centroids.shape
    return pl.pallas_call(
        cut_kernel,
        out_shape=jax.ShapeDtypeStruct((rows // 2, width), BF16),
        in_specs=[pl.BlockSpec(memory_space=VMEM)],
        out_specs=pl.BlockSpec(memory_space=VMEM),
        compiler_params=pltpu.CompilerParams(vmem_limit_bytes=2 << 20),
        cost_estimate=pl.CostEstimate(flops=1 << 20, bytes_accessed=1 << 20, transcendentals=0),
        name="cut",
    )(centroids)


def stage_kernel(feat_hbm, feat_ref, sem):
    copy = pltpu.make_async_copy(feat_hbm, feat_ref, sem)
    copy.start()
    copy.wait()


def staged(features):
    return pl.pallas_call(
        stage_kernel,
        out_shape=VMEM(features.shape, BF16),
        in_specs=[pl.BlockSpec(memory_space=pltpu.HBM)],
        out_specs=pl.BlockSpec(memory_space=VMEM),
        scratch_shapes=[pltpu.SemaphoreType.DMA(())],
        compiler_params=pltpu.CompilerParams(vmem_limit_bytes=1 << 20),
        cost_estimate=pl.CostEstimate(flops=1 << 30, bytes_accessed=5 << 20, transcendentals=0),
        name="staged",
    )(pltpu.with_memory_space_constraint(features, pltpu.HBM))


def square_kernel(feat_ref, sq_ref):
    frames, width = feat_ref.shape
    cell = 256
    eye = (
        lax.broadcasted_iota(jnp.int32, (cell, cell), 0) == lax.broadcasted_iota(jnp.int32, (cell, cell), 1)
    ).astype(BF16)
    for f in range(0, frames, cell):
        total = jnp.zeros((8, cell), F32)
        for k in range(0, width, cell):
            part = lax.dot_general(
                eye, feat_ref[f : f + cell, k : k + cell], (((1,), (1,)), ((), ())), preferred_element_type=F32
            )
            total = total + jnp.sum((part * part).reshape(cell // 8, 8, cell), axis=0)
        sq_ref[:, f : f + cell] = jnp.broadcast_to(jnp.sum(total, axis=0, keepdims=True), (8, cell))


def squares(features):
    frames, _ = features.shape
    return pl.pallas_call(
        square_kernel,
        out_shape=jax.ShapeDtypeStruct((8, frames), F32),
        in_specs=[pl.BlockSpec(memory_space=VMEM)],
        out_specs=pl.BlockSpec(memory_space=VMEM),
        compiler_params=pltpu.CompilerParams(vmem_limit_bytes=2 << 20),
        cost_estimate=pl.CostEstimate(flops=1 << 30, bytes_accessed=5 << 20, transcendentals=0),
        name="squares",
    )(features)


def score(cents, bases, own_ref, other_ref, least_in, index_in, least_ref, index_ref):
    rows = cents.shape[0] // len(bases)
    frames = own_ref.shape[0]
    tile = 256
    wide = cents.astype(F32)
    cent_sq = jnp.sum(wide * wide, axis=1, keepdims=True)
    scaled = cents * BF16(-2)
    sub = lax.broadcasted_iota(jnp.int32, (8, tile), 0)
    for side, feats in enumerate((own_ref, other_ref)):
        for f in range(0, frames, tile):
            at = slice(side * frames + f, side * frames + f + tile)
            dots = lax.dot_general(
                scaled, feats[f : f + tile], (((1,), (1,)), ((), ())), preferred_element_type=F32
            )
            least = index = None
            if least_in is not None:
                least, index = least_in[:, at], index_in[:, at]
            for block, base in enumerate(bases):
                low = where = None
                for r in range(0, rows, 8):
                    q = block * rows + r
                    value = dots[q : q + 8] + cent_sq[q : q + 8]
                    if low is None:
                        low, where = value, jnp.zeros((8, tile), jnp.int32)
                    else:
                        less = value < low
                        low = jnp.where(less, value, low)
                        where = jnp.where(less, r, where)
                where = where + (sub + base)
                if least is None:
                    least, index = low, where
                else:
                    better = (low < least) | ((low == least) & (where < index))
                    least = jnp.where(better, low, least)
                    index = jnp.where(better, where, index)
            least_ref[:, at] = least
            index_ref[:, at] = index


def pieces(value):
    high = value.astype(BF16)
    rest = value - high.astype(F32)
    middle = rest.astype(BF16)
    low = (rest - middle.astype(F32)).astype(BF16)
    return high, middle, low


def exact_dot(left, right):
    if left.dtype == F32:
        parts = [jnp.dot(p, right, preferred_element_type=F32) for p in pieces(left)]
    else:
        parts = [jnp.dot(left, p, preferred_element_type=F32) for p in pieces(right)]
    return (parts[0] + parts[1]) + parts[2]


def pack(least, index, square_ref, route_ref, other_route_ref, out_ref):
    frames = least.shape[1] // 2
    low = jnp.min(least, axis=0, keepdims=True)
    label = jnp.min(jnp.where(least == low, index, BIG), axis=0, keepdims=True).astype(F32)
    square = square_ref[0:1, :]
    sub = lax.broadcasted_iota(jnp.int32, (8, 128), 0)
    lane = lax.broadcasted_iota(jnp.int32, (8, 128), 1)
    mask = (lane // 16) == sub
    src = lax.broadcasted_iota(jnp.int32, (128, 128), 0)
    dst = lax.broadcasted_iota(jnp.int32, (128, 128), 1)

    def spread(row):
        groups = [
            jnp.where(mask, jnp.broadcast_to(row[:, i : i + 128], (8, 128)), 0.0) for i in range(0, frames, 128)
        ]
        return jnp.concatenate(groups, axis=0)

    def place(row, slot):
        pick = (dst == slot * 16 + lax.rem(src, 16)).astype(BF16)
        return exact_dot(spread(row), pick)

    own = place(low[:, :frames], 0) + place(label[:, :frames], 1) + place(square, 4)
    other = place(low[:, frames:], 2) + place(label[:, frames:], 3)
    to_own = (src == route_ref[0:1, :]).astype(BF16)
    to_other = (src == other_route_ref[0:1, :]).astype(BF16)
    out_ref[...] = exact_dot(to_own, own) + exact_dot(to_other, other)


def first_kernel(row, pair, own, other, least_ref, index_ref):
    rows = row.shape[0] // SIDE
    cents = jnp.concatenate([row[...], pair[...]], axis=0)
    score(cents, row_bases(0, rows) + pair_bases(True, rows), own, other, None, None, least_ref, index_ref)


def next_kernel(row, own, other, least_in, index_in, least_ref, index_ref):
    score(row[...], row_bases(1, row.shape[0] // SIDE), own, other, least_in, index_in, least_ref, index_ref)


def last_kernel(
    row, pair, own, other, least_in, index_in, square, route, other_route, out_ref, least_ref, index_ref
):
    rows = row.shape[0] // SIDE
    cents = jnp.concatenate([row[...], pair[...]], axis=0)
    bases = row_bases(-1, rows) + pair_bases(False, rows)
    score(cents, bases, own, other, least_in, index_in, least_ref, index_ref)
    pack(least_ref[...], index_ref[...], square, route, other_route, out_ref)


def scoring(kernel, args, out_shape, scratch=()):
    return pl.pallas_call(
        kernel,
        out_shape=out_shape,
        in_specs=[pl.BlockSpec(memory_space=VMEM)] * len(args),
        out_specs=jax.tree.map(lambda _: pl.BlockSpec(memory_space=VMEM), out_shape),
        scratch_shapes=list(scratch),
        compiler_params=pltpu.CompilerParams(vmem_limit_bytes=5 << 20),
        cost_estimate=pl.CostEstimate(flops=2 * 256 * 1280 * 4096, bytes_accessed=11 << 20, transcendentals=0),
    )(*args)


def merge_kernel(got_ref, label_ref, dist_ref, *, width):
    got = got_ref[...]
    turned = jnp.concatenate([got[r ^ 16 : (r ^ 16) + 16] for r in range(0, got.shape[0], 16)], axis=0)
    mine, theirs = got.T, turned.T
    low, label = mine[0:16], mine[16:32]
    other_low, other_label = theirs[32:48], theirs[48:64]
    better = (other_low < low) | ((other_low == low) & (other_label < label))
    label_ref[...] = jnp.where(better, other_label, label).astype(jnp.int32)
    dist_ref[...] = (mine[64:80] + jnp.where(better, other_low, low)) / width


def send(value, pairs):
    return lax.ppermute(value, AXES, pairs)


def labelled(features, centroids, route):
    frames, width = features.shape
    mine = cut(centroids)
    near = [mine] + [send(mine, along(o, 0)) for o in OFFSETS if o]
    pair = jnp.concatenate([send(mine, fetch(i)) for i in range(2)], axis=0)
    own = staged(features)
    other = send(features, core_swap())
    other_route = send(route, core_swap())
    square = squares(own)
    row = jnp.concatenate(near, axis=0)
    row_up = send(row, along(1, 1))
    row_down = send(row, along(-1, 1))
    other_pair = send(pair, plane_swap())
    state = (jax.ShapeDtypeStruct((8, 2 * frames), F32), jax.ShapeDtypeStruct((8, 2 * frames), jnp.int32))
    least, index = scoring(first_kernel, (row, pair, own, other), state)
    least, index = scoring(next_kernel, (row_up, own, other, least, index), state)
    packed = scoring(
        last_kernel,
        (row_down, other_pair, own, other, least, index, square, route, other_route),
        jax.ShapeDtypeStruct((128, 128), F32),
        scratch=[pltpu.VMEM((8, 2 * frames), F32), pltpu.VMEM((8, 2 * frames), jnp.int32)],
    )
    got = lax.all_to_all(packed, AXES, split_axis=0, concat_axis=0, tiled=True)
    label, dist = pl.pallas_call(
        functools.partial(merge_kernel, width=float(width)),
        out_shape=(jax.ShapeDtypeStruct((16, 128), jnp.int32), jax.ShapeDtypeStruct((16, 128), F32)),
        in_specs=[pl.BlockSpec(memory_space=VMEM)],
        out_specs=(pl.BlockSpec(memory_space=VMEM),) * 2,
        compiler_params=pltpu.CompilerParams(vmem_limit_bytes=2 << 20),
        name="merge",
    )(got)
    return label.T[None], dist.T[None]


def solution(mesh):
    placed = (P(AXES, None), P("clu", None), P(AXES, None))
    return jax.shard_map(
        labelled,
        mesh=mesh,
        in_specs=placed,
        out_specs=(P(AXES, None, None), P(AXES, None, None)),
        check_vma=False,
    )
```

profile of v0, /device:TPU:1, one launch (start us, length us, event | category | flops | bytes accessed | tf_op | source)
XLA Modules:
  0.0 56.8 jit_solution(3839404587710873195)
XLA Ops:
  0.6 1.5 %collective-permute-start.7 = (bf16[2048,1280]{1,0:T(8,128)(2,1)}, bf16[2048,1280]{1,0:T(8,128)(2,1)S(1)}, u32[]{:S(2)}, u32[]{:S(2)}) collective-permute-start(bf16[2048,1280]{1,0:T(8,128)(2,1)} %feat_hbm.1), channel_id=1, source_target_pairs={{0,16},{1,17},{2,18},{3,19},{4,20},{5,21},{6,22},{7,23},{8,24},{9,... | collective-permute-start | bytes 15728648 | tf_op jit(solution)/shard_map/ppermute | solution.py:281
  2.1 1.0 %copy-done = bf16[128,1280]{1,0:T(8,128)(2,1)S(1)} copy-done((bf16[128,1280]{1,0:T(8,128)(2,1)S(1)}, bf16[128,1280]{1,0:T(8,128)(2,1)}, u32[]{:S(2)}) %copy-start) | copy-done | bytes 327704
  3.1 1.8 %collective-permute-start = (bf16[64,1280]{1,0:T(8,128)(2,1)S(1)}, bf16[64,1280]{1,0:T(8,128)(2,1)S(1)}, u32[]{:S(2)}, u32[]{:S(2)}) collective-permute-start(bf16[64,1280]{1,0:T(8,128)(2,1)S(1)} %cut.1), channel_id=1, source_target_pairs={{0,1},{1,2},{2,3},{3,0},{4,5},{5,6},{6,7},{7,4},{8,9},{9,10},{10,1... | collective-permute-start | bytes 491528 | tf_op jit(solution)/shard_map/ppermute | solution.py:281
  4.9 2.2 %collective-permute-start.1 = (bf16[64,1280]{1,0:T(8,128)(2,1)S(1)}, bf16[64,1280]{1,0:T(8,128)(2,1)S(1)}, u32[]{:S(2)}, u32[]{:S(2)}) collective-permute-start(bf16[64,1280]{1,0:T(8,128)(2,1)S(1)} %cut.1), channel_id=1, source_target_pairs={{0,3},{1,0},{2,1},{3,2},{4,7},{5,4},{6,5},{7,6},{8,11},{9,8},{10,9... | collective-permute-start | bytes 491528 | tf_op jit(solution)/shard_map/ppermute | solution.py:281
  7.1 1.2 %collective-permute-start.2 = (bf16[64,1280]{1,0:T(8,128)(2,1)S(1)}, bf16[64,1280]{1,0:T(8,128)(2,1)S(1)}, u32[]{:S(2)}, u32[]{:S(2)}) collective-permute-start(bf16[64,1280]{1,0:T(8,128)(2,1)S(1)} %cut.1), channel_id=1, source_target_pairs={{0,2},{1,3},{2,0},{3,1},{4,6},{5,7},{6,4},{7,5},{8,10},{9,11},{10,... | collective-permute-start | bytes 491528 | tf_op jit(solution)/shard_map/ppermute | solution.py:281
  8.3 2.7 %collective-permute-start.4 = (bf16[64,1280]{1,0:T(8,128)(2,1)S(1)}, bf16[64,1280]{1,0:T(8,128)(2,1)S(1)}, u32[]{:S(2)}, u32[]{:S(2)}) collective-permute-start(bf16[64,1280]{1,0:T(8,128)(2,1)S(1)} %cut.1), channel_id=1, source_target_pairs={{0,8},{1,9},{2,10},{3,11},{4,12},{5,13},{6,14},{7,15},{8,0},{9,1},... | collective-permute-start | bytes 491528 | tf_op jit(solution)/shard_map/ppermute | solution.py:281
  11.1 2.5 %staged.1.own.feat_ref = bf16[2048,1280]{1,0:T(8,128)(2,1)S(1)} custom-call(bf16[2048,1280]{1,0:T(8,128)(2,1)} %feat_hbm.1), custom_call_target="tpu_custom_call" | custom-call | flops 1073741824 | bytes 5242880 | tf_op jit(solution)/shard_map/staged/pallas_call | solution.py:113
  13.6 0.0 copy-start.1
  13.6 1.6 %squares.1.square = f32[8,2048]{1,0:T(8,128)S(1)} custom-call(bf16[2048,1280]{1,0:T(8,128)(2,1)S(1)} %staged.1.own.feat_ref), custom_call_target="tpu_custom_call" | custom-call | flops 1073741824 | bytes 5242880 | tf_op jit(solution)/shard_map/squares/pallas_call | solution.py:143
  15.2 0.0 collective-permute-done
  15.2 1.8 %collective-permute-start.5 = (bf16[64,1280]{1,0:T(8,128)(2,1)S(1)}, bf16[64,1280]{1,0:T(8,128)(2,1)S(1)}, u32[]{:S(2)}, u32[]{:S(2)}) collective-permute-start(bf16[64,1280]{1,0:T(8,128)(2,1)S(1)} %cut.1), channel_id=1, source_target_pairs={{0,10},{1,11},{2,8},{3,9},{4,14},{5,15},{6,12},{7,13},{8,2},{9,3},... | collective-permute-start | bytes 491528 | tf_op jit(solution)/shard_map/ppermute | solution.py:281
  16.9 0.0 collective-permute-done.1
  16.9 0.6 %collective-permute-start.9 = (s32[1,128]{1,0:T(1,128)S(1)}, s32[1,128]{1,0:T(1,128)S(1)}, u32[]{:S(2)}, u32[]{:S(2)}) collective-permute-start(s32[1,128]{1,0:T(1,128)S(1)} %copy-done.1), channel_id=1, source_target_pairs={{0,16},{1,17},{2,18},{3,19},{4,20},{5,21},{6,22},{7,23},{8,24},{9,... | collective-permute-start | bytes 1544 | tf_op jit(solution)/shard_map/ppermute | solution.py:281
  17.5 0.0 collective-permute-done.2
  17.6 0.7 %collective-permute-start.8 = (bf16[256,1280]{1,0:T(8,128)(2,1)S(1)}, bf16[256,1280]{1,0:T(8,128)(2,1)S(1)}, u32[]{:S(2)}, u32[]{:S(2)}) collective-permute-start(bf16[256,1280]{1,0:T(8,128)(2,1)S(1)} %pad_maximum_fusion.row), channel_id=1, source_target_pairs={{0,4},{1,5},{2,6},{3,7},{4,8},{5,9},{6,10},{7,11},{8,12},{9,13},{1... | collective-permute-start | bytes 1966088 | tf_op jit(solution)/shard_map/ppermute | solution.py:281
  18.3 2.1 %collective-permute-start.3 = (bf16[256,1280]{1,0:T(8,128)(2,1)S(1)}, bf16[256,1280]{1,0:T(8,128)(2,1)S(1)}, u32[]{:S(2)}, u32[]{:S(2)}) collective-permute-start(bf16[256,1280]{1,0:T(8,128)(2,1)S(1)} %pad_maximum_fusion.row), channel_id=1, source_target_pairs={{0,12},{1,13},{2,14},{3,15},{4,0},{5,1},{6,2},{7,3},{8,4},{9,5},{1... | collective-permute-start | bytes 1966088 | tf_op jit(solution)/shard_map/ppermute | solution.py:281
  20.4 3.4 %collective-permute-done.5 = bf16[64,1280]{1,0:T(8,128)(2,1)S(1)} collective-permute-done((bf16[64,1280]{1,0:T(8,128)(2,1)S(1)}, bf16[64,1280]{1,0:T(8,128)(2,1)S(1)}, u32[]{:S(2)}, u32[]{:S(2)}) %collective-permute-start.5) | collective-permute-done | bytes 163872 | tf_op jit(solution)/shard_map/ppermute | solution.py:281
  23.8 1.8 %collective-permute-start.6 = (bf16[128,1280]{1,0:T(8,128)(2,1)S(1)}, bf16[128,1280]{1,0:T(8,128)(2,1)S(1)}, u32[]{:S(2)}, u32[]{:S(2)}) collective-permute-start(bf16[128,1280]{1,0:T(8,128)(2,1)S(1)} %constant_dynamic-update-slice_fusion.pair), channel_id=1, source_target_pairs={{0,32},{1,33},{2,34},{3,35},{4,36},{5,37},{6,38},{7,39},{8,40},{9,... | collective-permute-start | bytes 983048 | tf_op jit(solution)/shard_map/ppermute | solution.py:281
  25.6 4.4 %shard_map.50 = (f32[8,4096]{1,0:T(8,128)S(1)}, s32[8,4096]{1,0:T(8,128)S(1)}) custom-call(bf16[256,1280]{1,0:T(8,128)(2,1)S(1)} %pad_maximum_fusion.row, bf16[128,1280]{1,0:T(8,128)(2,1)S(1)} %constant_dynamic-update-slice_fusion.pair, bf16[2048,1280]{1,0:T(8,128)(2,1)S(1)} %staged.1.own.feat_ref, bf16[2048,1280]{1,0:T(8,128)(2,1)S(1)} %collective-permute-done.7.other), custom_call_target="tpu_custom_call" | custom-call | flops 2684354560 | bytes 11534336 | tf_op jit(solution)/shard_map/pallas_call | solution.py:258
  30.0 1.1 %collective-permute-done.8.row = bf16[256,1280]{1,0:T(8,128)(2,1)S(1)} collective-permute-done((bf16[256,1280]{1,0:T(8,128)(2,1)S(1)}, bf16[256,1280]{1,0:T(8,128)(2,1)S(1)}, u32[]{:S(2)}, u32[]{:S(2)}) %collective-permute-start.8) | collective-permute-done | bytes 655392 | tf_op jit(solution)/shard_map/ppermute | solution.py:281
  31.0 3.1 %shard_map.51 = (f32[8,4096]{1,0:T(8,128)S(1)}, s32[8,4096]{1,0:T(8,128)S(1)}) custom-call(bf16[256,1280]{1,0:T(8,128)(2,1)S(1)} %collective-permute-done.8.row, bf16[2048,1280]{1,0:T(8,128)(2,1)S(1)} %staged.1.own.feat_ref, bf16[2048,1280]{1,0:T(8,128)(2,1)S(1)} %collective-permute-done.7.other, f32[8,4096]{1,0:T(8,128)S(1)} %get-tuple-element.8.least_in, ...), custom_call_target="tpu_custom_call" | custom-call | flops 2684354560 | bytes 11534336 | tf_op jit(solution)/shard_map/pallas_call | solution.py:258
  34.1 4.8 %shard_map.52 = f32[128,128]{1,0:T(8,128)S(1)} custom-call(bf16[256,1280]{1,0:T(8,128)(2,1)S(1)} %collective-permute-done.3.row, bf16[128,1280]{1,0:T(8,128)(2,1)S(1)} %collective-permute-done.6.pair, bf16[2048,1280]{1,0:T(8,128)(2,1)S(1)} %staged.1.own.feat_ref, bf16[2048,1280]{1,0:T(8,128)(2,1)S(1)} %collective-permute-done.7.other, ...), custom_call_target="tpu_custom_call" | custom-call | flops 2684354560 | bytes 11534336 | tf_op jit(solution)/shard_map/pallas_call | solution.py:258
  38.9 17.2 %all_to_all.11 = f32[128,1,128]{2,1,0:T(1,128)S(1)} all-to-all(f32[128,1,128]{2,1,0:T(1,128)S(1)} %bitcast.10), channel_id=1, replica_groups=mesh['utt'=8,'clu'=16] {'utt','clu'}, dimensions={0} | all-to-all | bytes 131072 | tf_op jit(solution)/shard_map/all_to_all | solution.py:306
  56.1 0.7 %merge.1 = (s32[16,128]{1,0:T(8,128)}, f32[16,128]{1,0:T(8,128)}) custom-call(f32[128,128]{1,0:T(8,128)S(1)} %bitcast.11), custom_call_target="tpu_custom_call" | custom-call | tf_op jit(solution)/shard_map/merge/pallas_call | solution.py:307
  (11 shorter events, 0.1 us)
Async XLA Ops:
  0.6 25.0 %collective-permute-start.7 = (bf16[2048,1280]{1,0:T(8,128)(2,1)}, bf16[2048,1280]{1,0:T(8,128)(2,1)S(1)}, u32[]{:S(2)}, u32[]{:S(2)}) collective-permute-start(bf16[2048,1280]{1,0:T(8,128)(2,1)} %feat_hbm.1), channel_id=1, source_target_pairs={{0,16},{1,17},{2,18},{3,19},{4,20},{5,21},{6,22},{7,23},{8,24},{9,... | collective-permute-start | bytes 15728648 | tf_op jit(solution)/shard_map/ppermute | solution.py:281
  2.1 1.0 %copy-start = (bf16[128,1280]{1,0:T(8,128)(2,1)S(1)}, bf16[128,1280]{1,0:T(8,128)(2,1)}, u32[]{:S(2)}) copy-start(bf16[128,1280]{1,0:T(8,128)(2,1)} %cents_ref.1) | copy-start | bytes 983044
  3.1 12.1 %collective-permute-start = (bf16[64,1280]{1,0:T(8,128)(2,1)S(1)}, bf16[64,1280]{1,0:T(8,128)(2,1)S(1)}, u32[]{:S(2)}, u32[]{:S(2)}) collective-permute-start(bf16[64,1280]{1,0:T(8,128)(2,1)S(1)} %cut.1), channel_id=1, source_target_pairs={{0,1},{1,2},{2,3},{3,0},{4,5},{5,6},{6,7},{7,4},{8,9},{9,10},{10,1... | collective-permute-start | bytes 491528 | tf_op jit(solution)/shard_map/ppermute | solution.py:281
  4.9 12.0 %collective-permute-start.1 = (bf16[64,1280]{1,0:T(8,128)(2,1)S(1)}, bf16[64,1280]{1,0:T(8,128)(2,1)S(1)}, u32[]{:S(2)}, u32[]{:S(2)}) collective-permute-start(bf16[64,1280]{1,0:T(8,128)(2,1)S(1)} %cut.1), channel_id=1, source_target_pairs={{0,3},{1,0},{2,1},{3,2},{4,7},{5,4},{6,5},{7,6},{8,11},{9,8},{10,9... | collective-permute-start | bytes 491528 | tf_op jit(solution)/shard_map/ppermute | solution.py:281
  7.1 10.4 %collective-permute-start.2 = (bf16[64,1280]{1,0:T(8,128)(2,1)S(1)}, bf16[64,1280]{1,0:T(8,128)(2,1)S(1)}, u32[]{:S(2)}, u32[]{:S(2)}) collective-permute-start(bf16[64,1280]{1,0:T(8,128)(2,1)S(1)} %cut.1), channel_id=1, source_target_pairs={{0,2},{1,3},{2,0},{3,1},{4,6},{5,7},{6,4},{7,5},{8,10},{9,11},{10,... | collective-permute-start | bytes 491528 | tf_op jit(solution)/shard_map/ppermute | solution.py:281
  8.3 10.0 %collective-permute-start.4 = (bf16[64,1280]{1,0:T(8,128)(2,1)S(1)}, bf16[64,1280]{1,0:T(8,128)(2,1)S(1)}, u32[]{:S(2)}, u32[]{:S(2)}) collective-permute-start(bf16[64,1280]{1,0:T(8,128)(2,1)S(1)} %cut.1), channel_id=1, source_target_pairs={{0,8},{1,9},{2,10},{3,11},{4,12},{5,13},{6,14},{7,15},{8,0},{9,1},... | collective-permute-start | bytes 491528 | tf_op jit(solution)/shard_map/ppermute | solution.py:281
  13.6 3.4 %copy-start.1 = (s32[1,128]{1,0:T(1,128)S(1)}, s32[1,128]{1,0:T(1,128)}, u32[]{:S(2)}) copy-start(s32[1,128]{1,0:T(1,128)} %route.1) | copy-start | bytes 1540
  15.2 8.6 %collective-permute-start.5 = (bf16[64,1280]{1,0:T(8,128)(2,1)S(1)}, bf16[64,1280]{1,0:T(8,128)(2,1)S(1)}, u32[]{:S(2)}, u32[]{:S(2)}) collective-permute-start(bf16[64,1280]{1,0:T(8,128)(2,1)S(1)} %cut.1), channel_id=1, source_target_pairs={{0,10},{1,11},{2,8},{3,9},{4,14},{5,15},{6,12},{7,13},{8,2},{9,3},... | collective-permute-start | bytes 491528 | tf_op jit(solution)/shard_map/ppermute | solution.py:281
  16.9 17.2 %collective-permute-start.9 = (s32[1,128]{1,0:T(1,128)S(1)}, s32[1,128]{1,0:T(1,128)S(1)}, u32[]{:S(2)}, u32[]{:S(2)}) collective-permute-start(s32[1,128]{1,0:T(1,128)S(1)} %copy-done.1), channel_id=1, source_target_pairs={{0,16},{1,17},{2,18},{3,19},{4,20},{5,21},{6,22},{7,23},{8,24},{9,... | collective-permute-start | bytes 1544 | tf_op jit(solution)/shard_map/ppermute | solution.py:281
  17.6 13.4 %collective-permute-start.8 = (bf16[256,1280]{1,0:T(8,128)(2,1)S(1)}, bf16[256,1280]{1,0:T(8,128)(2,1)S(1)}, u32[]{:S(2)}, u32[]{:S(2)}) collective-permute-start(bf16[256,1280]{1,0:T(8,128)(2,1)S(1)} %pad_maximum_fusion.row), channel_id=1, source_target_pairs={{0,4},{1,5},{2,6},{3,7},{4,8},{5,9},{6,10},{7,11},{8,12},{9,13},{1... | collective-permute-start | bytes 1966088 | tf_op jit(solution)/shard_map/ppermute | solution.py:281
  18.3 15.8 %collective-permute-start.3 = (bf16[256,1280]{1,0:T(8,128)(2,1)S(1)}, bf16[256,1280]{1,0:T(8,128)(2,1)S(1)}, u32[]{:S(2)}, u32[]{:S(2)}) collective-permute-start(bf16[256,1280]{1,0:T(8,128)(2,1)S(1)} %pad_maximum_fusion.row), channel_id=1, source_target_pairs={{0,12},{1,13},{2,14},{3,15},{4,0},{5,1},{6,2},{7,3},{8,4},{9,5},{1... | collective-permute-start | bytes 1966088 | tf_op jit(solution)/shard_map/ppermute | solution.py:281
  23.8 10.3 %collective-permute-start.6 = (bf16[128,1280]{1,0:T(8,128)(2,1)S(1)}, bf16[128,1280]{1,0:T(8,128)(2,1)S(1)}, u32[]{:S(2)}, u32[]{:S(2)}) collective-permute-start(bf16[128,1280]{1,0:T(8,128)(2,1)S(1)} %constant_dynamic-update-slice_fusion.pair), channel_id=1, source_target_pairs={{0,32},{1,33},{2,34},{3,35},{4,36},{5,37},{6,38},{7,39},{8,40},{9,... | collective-permute-start | bytes 983048 | tf_op jit(solution)/shard_map/ppermute | solution.py:281
where the time goes:
time: 57 us; the launch traced here: 56.8 us
  blocking collectives  17.2 us (30%)
  Pallas kernels  17 us (30%)
  starting transfers between devices  16.4 us (29%)
  waiting for transfers between devices  4.49 us (8%)
  local copies, waits for them, and re-layouts  1 us (2%)
  between operations  0.73 us (1%)
    all_to_all x1, blocking collectives, labelled(): got = lax.all_to_all(packed, AXES, split_axis=0, concat_axis=0, tiled=True)  17.2 us
    ppermute x10, starting transfers between devices, send(): return lax.ppermute(value, AXES, pairs)  16.4 us
    pallas_call x3, Pallas kernels, scoring(): pl.pallas_call(kernel, out_shape=out_shape, in_specs=[pl.BlockSpec(memory...  12.2 us
    ppermute x10, waiting for transfers between devices, send(): return lax.ppermute(value, AXES, pairs)  4.49 us
    pallas_call x1, Pallas kernels, staged(): pl.pallas_call(stage_kernel, out_shape=VMEM(features.shape, BF16), in_spe...  2.49 us
    pallas_call x1, Pallas kernels, squares(): pl.pallas_call(square_kernel, out_shape=jax.ShapeDtypeStruct((8, frames),...  1.57 us
  transfers between devices with their start and end apart: 10, of which 2 were waited for; matrix products, arithmetic and copies ran while one was open for 0% of the time, Pallas kernels for 20%

commit v1 on v0

--- a/solution.py
+++ b/solution.py
@@ -10,7 +10,6 @@
 
 AXES = ("utt", "clu")
 SIDE = 4
-OFFSETS = (0, 1, -1, 2)
 VMEM = pltpu.VMEM
 F32 = jnp.float32
 BF16 = jnp.bfloat16
@@ -21,105 +20,73 @@
     return (y * 2 + c) * 16 + (z % SIDE) * SIDE + x % SIDE
 
 
-def along(offset, phase):
-    pairs = []
-    for y in range(4):
-        for c in range(2):
-            for z in range(SIDE):
-                for x in range(SIDE):
-                    on_x = (c == 0) == (phase == 0)
-                    target = device(y, c, z, x + offset) if on_x else device(y, c, z + offset, x)
-                    pairs.append((device(y, c, z, x), target))
-    return pairs
-
-
-def core_swap():
+def everywhere(target):
+    def at(y, c, near, far):
+        return device(y, c, far, near) if c == 0 else device(y, c, near, far)
+
     return [
-        (device(y, c, z, x), device(y, 1 - c, z, x))
+        (at(y, c, near, far), at(*target(y, c, near, far)))
         for y in range(4)
         for c in range(2)
-        for z in range(SIDE)
-        for x in range(SIDE)
+        for near in range(SIDE)
+        for far in range(SIDE)
     ]
 
 
-def fetch(step):
-    pairs = []
-    for y in range(4):
-        for c in range(2):
-            for z in range(SIDE):
-                for x in range(SIDE):
-                    near = y % 2 + 2 * step
-                    target = device(y, c, z - 2, x - near) if c == 0 else device(y, c, z - near, x - 2)
-                    pairs.append((device(y, c, z, x), target))
-    return pairs
-
-
-def plane_swap():
-    return [
-        (device(y, c, z, x), device(y ^ 1, c, z, x))
-        for y in range(4)
-        for c in range(2)
-        for z in range(SIDE)
-        for x in range(SIDE)
-    ]
-
-
-def block_base(far, near, rows):
+def near_step(offset):
+    return everywhere(lambda y, c, near, far: (y, c, near + offset, far))
+
+
+def far_step(offset):
+    return everywhere(lambda y, c, near, far: (y, c, near, far + offset))
+
+
+def core_swap():
+    return everywhere(lambda y, c, near, far: (y, 1 - c, far, near))
+
+
+def place():
     core = lax.rem(lax.axis_index("utt"), 2)
     clu = lax.axis_index("clu")
     z, x = clu // SIDE, lax.rem(clu, SIDE)
-    from_z = lax.rem(z + jnp.where(core == 0, far, near), SIDE)
-    from_x = lax.rem(x + jnp.where(core == 0, near, far), SIDE)
-    return (from_z * SIDE + from_x) * (2 * rows) + core * rows
-
-
-def row_bases(far, rows):
-    return [block_base((SIDE - far) % SIDE, (SIDE - near) % SIDE, rows) for near in OFFSETS]
-
-
-def pair_bases(own, rows):
-    plane = lax.rem(lax.axis_index("utt") // 2, 2)
-    first = plane if own else 1 - plane
-    return [block_base(2, lax.rem(first + 2 * step, SIDE), rows) for step in range(2)]
-
-
-def cut_kernel(cents_ref, out_ref):
+    return core, jnp.where(core == 0, x, z), jnp.where(core == 0, z, x)
+
+
+def half_bases(near_offsets, far_offset, rows):
+    core, near, far = place()
+    bases = []
+    for offset in near_offsets:
+        n = lax.rem(near + SIDE + offset, SIDE)
+        f = lax.rem(far + SIDE + far_offset, SIDE)
+        shard = jnp.where(core == 0, f * SIDE + n, n * SIDE + f)
+        bases.append(shard * (2 * rows) + core * rows)
+    return bases
+
+
+FIRST = (0, -1)
+SECOND = (1, -2)
+
+
+def cut_kernel(cents_hbm, out_ref, sem):
     rows = out_ref.shape[0]
     core = lax.rem(lax.axis_index("utt"), 2)
-    out_ref[...] = cents_ref[pl.ds(pl.multiple_of(core * rows, rows), rows), :]
+    copy = pltpu.make_async_copy(cents_hbm.at[pl.ds(pl.multiple_of(core * rows, rows), rows)], out_ref, sem)
+    copy.start()
+    copy.wait()
 
 
 def cut(centroids):
     rows, width = centroids.shape
     return pl.pallas_call(
         cut_kernel,
-        out_shape=jax.ShapeDtypeStruct((rows // 2, width), BF16),
-        in_specs=[pl.BlockSpec(memory_space=VMEM)],
-        out_specs=pl.BlockSpec(memory_space=VMEM),
-        compiler_params=pltpu.CompilerParams(vmem_limit_bytes=2 << 20),
-        cost_estimate=pl.CostEstimate(flops=1 << 20, bytes_accessed=1 << 20, transcendentals=0),
-        name="cut",
-    )(centroids)
-
-
-def stage_kernel(feat_hbm, feat_ref, sem):
-    copy = pltpu.make_async_copy(feat_hbm, feat_ref, sem)
-    copy.start()
-    copy.wait()
-
-
-def staged(features):
-    return pl.pallas_call(
-        stage_kernel,
-        out_shape=VMEM(features.shape, BF16),
+        out_shape=VMEM((rows // 2, width), BF16),
         in_specs=[pl.BlockSpec(memory_space=pltpu.HBM)],
         out_specs=pl.BlockSpec(memory_space=VMEM),
         scratch_shapes=[pltpu.SemaphoreType.DMA(())],
         compiler_params=pltpu.CompilerParams(vmem_limit_bytes=1 << 20),
-        cost_estimate=pl.CostEstimate(flops=1 << 30, bytes_accessed=5 << 20, transcendentals=0),
-        name="staged",
-    )(pltpu.with_memory_space_constraint(features, pltpu.HBM))
+        cost_estimate=pl.CostEstimate(flops=1 << 34, bytes_accessed=1 << 20, transcendentals=0),
+        name="cut",
+    )(pltpu.with_memory_space_constraint(centroids, pltpu.HBM))
 
 
 def square_kernel(feat_ref, sq_ref):
@@ -234,22 +201,26 @@
     out_ref[...] = exact_dot(to_own, own) + exact_dot(to_other, other)
 
 
-def first_kernel(row, pair, own, other, least_ref, index_ref):
-    rows = row.shape[0] // SIDE
-    cents = jnp.concatenate([row[...], pair[...]], axis=0)
-    score(cents, row_bases(0, rows) + pair_bases(True, rows), own, other, None, None, least_ref, index_ref)
-
-
-def next_kernel(row, own, other, least_in, index_in, least_ref, index_ref):
-    score(row[...], row_bases(1, row.shape[0] // SIDE), own, other, least_in, index_in, least_ref, index_ref)
+def halves(first, first_from, second, second_from):
+    rows = first.shape[0] // 2
+    bases = half_bases(FIRST, first_from, rows) + half_bases(SECOND, second_from, rows)
+    return jnp.concatenate([first[...], second[...]], axis=0), bases
+
+
+def first_kernel(first, second, own, other, least_ref, index_ref):
+    cents, bases = halves(first, 0, second, 0)
+    score(cents, bases, own, other, None, None, least_ref, index_ref)
+
+
+def next_kernel(first_from, second_from, first, second, own, other, least_in, index_in, least_ref, index_ref):
+    cents, bases = halves(first, first_from, second, second_from)
+    score(cents, bases, own, other, least_in, index_in, least_ref, index_ref)
 
 
 def last_kernel(
-    row, pair, own, other, least_in, index_in, square, route, other_route, out_ref, least_ref, index_ref
+    first, second, own, other, least_in, index_in, square, route, other_route, out_ref, least_ref, index_ref
 ):
-    rows = row.shape[0] // SIDE
-    cents = jnp.concatenate([row[...], pair[...]], axis=0)
-    bases = row_bases(-1, rows) + pair_bases(False, rows)
+    cents, bases = halves(first, 2, second, 2)
     score(cents, bases, own, other, least_in, index_in, least_ref, index_ref)
     pack(least_ref[...], index_ref[...], square, route, other_route, out_ref)
 
@@ -283,23 +254,33 @@
 
 def labelled(features, centroids, route):
     frames, width = features.shape
-    mine = cut(centroids)
-    near = [mine] + [send(mine, along(o, 0)) for o in OFFSETS if o]
-    pair = jnp.concatenate([send(mine, fetch(i)) for i in range(2)], axis=0)
-    own = staged(features)
     other = send(features, core_swap())
     other_route = send(route, core_swap())
+    mine = cut(centroids)
+    near1 = send(mine, near_step(1))
+    near2 = send(mine, near_step(-1))
+    near3 = send(mine, near_step(2))
+    first = jnp.concatenate([mine, near1], axis=0)
+    second = jnp.concatenate([near2, near3], axis=0)
+    up_first = send(first, far_step(1))
+    down_second = send(second, far_step(-1))
+    up_second = send(second, far_step(1))
+    down_first = send(first, far_step(-1))
+    over_first = send(up_first, far_step(1))
+    over_second = send(down_second, far_step(-1))
+    own = pltpu.with_memory_space_constraint(features, VMEM)
     square = squares(own)
-    row = jnp.concatenate(near, axis=0)
-    row_up = send(row, along(1, 1))
-    row_down = send(row, along(-1, 1))
-    other_pair = send(pair, plane_swap())
     state = (jax.ShapeDtypeStruct((8, 2 * frames), F32), jax.ShapeDtypeStruct((8, 2 * frames), jnp.int32))
-    least, index = scoring(first_kernel, (row, pair, own, other), state)
-    least, index = scoring(next_kernel, (row_up, own, other, least, index), state)
+    least, index = scoring(first_kernel, (first, second, own, other), state)
+    least, index = scoring(
+        functools.partial(next_kernel, -1, 1), (up_first, down_second, own, other, least, index), state
+    )
+    least, index = scoring(
+        functools.partial(next_kernel, 1, -1), (down_first, up_second, own, other, least, index), state
+    )
     packed = scoring(
         last_kernel,
-        (row_down, other_pair, own, other, least, index, square, route, other_route),
+        (over_first, over_second, own, other, least, index, square, route, other_route),
         jax.ShapeDtypeStruct((128, 128), F32),
         scratch=[pltpu.VMEM((8, 2 * frames), F32), pltpu.VMEM((8, 2 * frames), jnp.int32)],
     )

time: 57 us -> 56.1 us (0.984)
  Pallas kernels: 17 us -> 15.5 us
  blocking collectives: 17.2 us -> 18.5 us
  waiting for transfers between devices: 4.49 us -> 5.57 us
  local copies, waits for them, and re-layouts: 1 us -> 0.03 us
  starting transfers between devices: 16.4 us -> 15.6 us
    pallas_call x2 -> x1, Pallas kernels: 2.51 us -> 1.01 us  [cut(): pl.pallas_call(cut_kernel, out_shape=VMEM((rows // 2, width), BF16), in_s...]
    all_to_all x1, blocking collectives: 17.2 us -> 18.5 us  [labelled(): got = lax.all_to_all(packed, AXES, split_axis=0, concat_axis=0, tiled=True)]
    ppermute x10 -> x11, waiting for transfers between devices: 4.49 us -> 5.57 us  [send(): return lax.ppermute(value, AXES, pairs)]
    unnamed x5, local copies, waits for them, and re-layouts: 0.99 us -> 0.02 us
    ppermute x10 -> x11, starting transfers between devices: 16.4 us -> 15.6 us  [send(): return lax.ppermute(value, AXES, pairs)]
    pallas_call x3 -> x4, Pallas kernels: 12.2 us -> 12.2 us  [scoring(): pl.pallas_call(kernel, out_shape=out_shape, in_specs=[pl.BlockSpec(memory...]
  transfers between devices with their start and end apart: 10 -> 11, of which waited for: 2 -> 4; matrix products, arithmetic and copies ran while one was open for 0% -> 0% of each run, Pallas kernels for 20% -> 20%
where the time goes in v1:
time: 56.1 us; the launch traced here: 55.9 us
  blocking collectives  18.5 us (33%)
  starting transfers between devices  15.6 us (28%)
  Pallas kernels  15.5 us (28%)
  waiting for transfers between devices  5.57 us (10%)
  between operations  0.77 us (1%)
    all_to_all x1, blocking collectives, labelled(): got = lax.all_to_all(packed, AXES, split_axis=0, concat_axis=0, tiled=True)  18.5 us
    ppermute x11, starting transfers between devices, send(): return lax.ppermute(value, AXES, pairs)  15.6 us
    pallas_call x4, Pallas kernels, scoring(): pl.pallas_call(kernel, out_shape=out_shape, in_specs=[pl.BlockSpec(memory...  12.2 us
    ppermute x11, waiting for transfers between devices, send(): return lax.ppermute(value, AXES, pairs)  5.57 us
    pallas_call x1, Pallas kernels, squares(): pl.pallas_call(square_kernel, out_shape=jax.ShapeDtypeStruct((8, frames),...  1.57 us
  transfers between devices with their start and end apart: 11, of which 4 were waited for; matrix products, arithmetic and copies ran while one was open for 0% of the time, Pallas kernels for 20%

profile of v1, /device:TPU:1, one launch (start us, length us, event | category | flops | bytes accessed | tf_op | source)
XLA Modules:
  0.0 55.9 jit_solution(1877957912307576627)
XLA Ops:
  0.6 1.5 %collective-permute-start.7 = (bf16[2048,1280]{1,0:T(8,128)(2,1)}, bf16[2048,1280]{1,0:T(8,128)(2,1)S(1)}, u32[]{:S(2)}, u32[]{:S(2)}) collective-permute-start(bf16[2048,1280]{1,0:T(8,128)(2,1)} %own.7), channel_id=1, source_target_pairs={{0,16},{4,20},{8,24},{12,28},{1,17},{5,21},{9,25},{13,29},{2,18},{... | collective-permute-start | bytes 15728648 | tf_op jit(solution)/shard_map/ppermute | solution.py:252
  2.1 1.0 %cut.1 = bf16[64,1280]{1,0:T(8,128)(2,1)S(1)} custom-call(bf16[128,1280]{1,0:T(8,128)(2,1)} %cents_hbm.1), custom_call_target="tpu_custom_call" | custom-call | flops 17179869184 | bytes 1048576 | tf_op jit(solution)/shard_map/cut/pallas_call | solution.py:80
  3.1 4.0 %collective-permute-start.3 = (bf16[64,1280]{1,0:T(8,128)(2,1)S(1)}, bf16[64,1280]{1,0:T(8,128)(2,1)S(1)}, u32[]{:S(2)}, u32[]{:S(2)}) collective-permute-start(bf16[64,1280]{1,0:T(8,128)(2,1)S(1)} %cut.1), channel_id=1, source_target_pairs={{0,3},{4,7},{8,11},{12,15},{1,0},{5,4},{9,8},{13,12},{2,1},{6,5},{... | collective-permute-start | bytes 491528 | tf_op jit(solution)/shard_map/ppermute | solution.py:252
  7.1 0.0 collective-permute-start.4
  7.1 0.7 %collective-permute-start = (bf16[64,1280]{1,0:T(8,128)(2,1)S(1)}, bf16[64,1280]{1,0:T(8,128)(2,1)S(1)}, u32[]{:S(2)}, u32[]{:S(2)}) collective-permute-start(bf16[64,1280]{1,0:T(8,128)(2,1)S(1)} %cut.1), channel_id=1, source_target_pairs={{0,1},{4,5},{8,9},{12,13},{1,2},{5,6},{9,10},{13,14},{2,3},{6,7},{... | collective-permute-start | bytes 491528 | tf_op jit(solution)/shard_map/ppermute | solution.py:252
  7.8 3.3 %collective-permute-done.3 = bf16[64,1280]{1,0:T(8,128)(2,1)S(1)} collective-permute-done((bf16[64,1280]{1,0:T(8,128)(2,1)S(1)}, bf16[64,1280]{1,0:T(8,128)(2,1)S(1)}, u32[]{:S(2)}, u32[]{:S(2)}) %collective-permute-start.3) | collective-permute-done | bytes 163872 | tf_op jit(solution)/shard_map/ppermute | solution.py:252
  11.2 1.7 %collective-permute-done.4 = bf16[64,1280]{1,0:T(8,128)(2,1)S(1)} collective-permute-done((bf16[64,1280]{1,0:T(8,128)(2,1)S(1)}, bf16[64,1280]{1,0:T(8,128)(2,1)S(1)}, u32[]{:S(2)}, u32[]{:S(2)}) %collective-permute-start.4) | collective-permute-done | bytes 163872 | tf_op jit(solution)/shard_map/ppermute | solution.py:252
  12.9 2.5 %collective-permute-start.5 = (bf16[128,1280]{1,0:T(8,128)(2,1)S(1)}, bf16[128,1280]{1,0:T(8,128)(2,1)S(1)}, u32[]{:S(2)}, u32[]{:S(2)}) collective-permute-start(bf16[128,1280]{1,0:T(8,128)(2,1)S(1)} %constant_dynamic-update-slice_fusion.second), channel_id=1, source_target_pairs={{0,12},{4,0},{8,4},{12,8},{1,13},{5,1},{9,5},{13,9},{2,14},{6,2},{... | collective-permute-start | bytes 983048 | tf_op jit(solution)/shard_map/ppermute | solution.py:252
  15.5 0.1 collective-permute-start.1
  15.6 1.8 %collective-permute-start.10 = (s32[1,128]{1,0:T(1,128)S(1)}, s32[1,128]{1,0:T(1,128)S(1)}, u32[]{:S(2)}, u32[]{:S(2)}) collective-permute-start(s32[1,128]{1,0:T(1,128)S(1)} %copy-done.1), channel_id=1, source_target_pairs={{0,16},{4,20},{8,24},{12,28},{1,17},{5,21},{9,25},{13,29},{2,18},{... | collective-permute-start | bytes 1544 | tf_op jit(solution)/shard_map/ppermute | solution.py:252
  17.4 1.6 %squares.1.square = f32[8,2048]{1,0:T(8,128)S(1)} custom-call(bf16[2048,1280]{1,0:T(8,128)(2,1)S(1)} %copy-done), custom_call_target="tpu_custom_call" | custom-call | flops 1073741824 | bytes 5242880 | tf_op jit(solution)/shard_map/squares/pallas_call | solution.py:110
  19.0 0.1 collective-permute-start.9
  19.1 0.4 collective-permute-done.5.second
  19.5 3.4 %collective-permute-start.8 = (bf16[128,1280]{1,0:T(8,128)(2,1)S(1)}, bf16[128,1280]{1,0:T(8,128)(2,1)S(1)}, u32[]{:S(2)}, u32[]{:S(2)}) collective-permute-start(bf16[128,1280]{1,0:T(8,128)(2,1)S(1)} %pad_maximum_fusion.first), channel_id=1, source_target_pairs={{0,12},{4,0},{8,4},{12,8},{1,13},{5,1},{9,5},{13,9},{2,14},{6,2},{... | collective-permute-start | bytes 983048 | tf_op jit(solution)/shard_map/ppermute | solution.py:252
  22.9 0.1 collective-permute-done.1.first
  23.0 0.1 collective-permute-start.6
  23.1 0.0 collective-permute-done.7.other
  23.1 1.4 %collective-permute-start.2 = (bf16[128,1280]{1,0:T(8,128)(2,1)S(1)}, bf16[128,1280]{1,0:T(8,128)(2,1)S(1)}, u32[]{:S(2)}, u32[]{:S(2)}) collective-permute-start(bf16[128,1280]{1,0:T(8,128)(2,1)S(1)} %collective-permute-done.1.first), channel_id=1, source_target_pairs={{0,4},{4,8},{8,12},{12,0},{1,5},{5,9},{9,13},{13,1},{2,6},{6,10},{... | collective-permute-start | bytes 983048 | tf_op jit(solution)/shard_map/ppermute | solution.py:252
  24.5 2.9 %shard_map.50 = (f32[8,4096]{1,0:T(8,128)S(1)}, s32[8,4096]{1,0:T(8,128)S(1)}) custom-call(bf16[128,1280]{1,0:T(8,128)(2,1)S(1)} %pad_maximum_fusion.first, bf16[128,1280]{1,0:T(8,128)(2,1)S(1)} %constant_dynamic-update-slice_fusion.second, bf16[2048,1280]{1,0:T(8,128)(2,1)S(1)} %copy-done, bf16[2048,1280]{1,0:T(8,128)(2,1)S(1)} %collective-permute-done.7.other), custom_call_target="tpu_custom_call" | custom-call | flops 2684354560 | bytes 11534336 | tf_op jit(solution)/shard_map/pallas_call | solution.py:229
  27.4 2.9 %shard_map.51 = (f32[8,4096]{1,0:T(8,128)S(1)}, s32[8,4096]{1,0:T(8,128)S(1)}) custom-call(bf16[128,1280]{1,0:T(8,128)(2,1)S(1)} %collective-permute-done.1.first, bf16[128,1280]{1,0:T(8,128)(2,1)S(1)} %collective-permute-done.5.second, bf16[2048,1280]{1,0:T(8,128)(2,1)S(1)} %copy-done, bf16[2048,1280]{1,0:T(8,128)(2,1)S(1)} %collective-permute-done.7.other, ...), custom_call_target="tpu_custom_call" | custom-call | flops 2684354560 | bytes 11534336 | tf_op jit(solution)/shard_map/pallas_call | solution.py:229
  30.4 2.9 %shard_map.52 = (f32[8,4096]{1,0:T(8,128)S(1)}, s32[8,4096]{1,0:T(8,128)S(1)}) custom-call(bf16[128,1280]{1,0:T(8,128)(2,1)S(1)} %collective-permute-done.8.first, bf16[128,1280]{1,0:T(8,128)(2,1)S(1)} %collective-permute-done.9.second, bf16[2048,1280]{1,0:T(8,128)(2,1)S(1)} %copy-done, bf16[2048,1280]{1,0:T(8,128)(2,1)S(1)} %collective-permute-done.7.other, ...), custom_call_target="tpu_custom_call" | custom-call | flops 2684354560 | bytes 11534336 | tf_op jit(solution)/shard_map/pallas_call | solution.py:229
  33.4 3.4 %shard_map.53 = f32[128,128]{1,0:T(8,128)S(1)} custom-call(bf16[128,1280]{1,0:T(8,128)(2,1)S(1)} %collective-permute-done.2.first, bf16[128,1280]{1,0:T(8,128)(2,1)S(1)} %collective-permute-done.6.second, bf16[2048,1280]{1,0:T(8,128)(2,1)S(1)} %copy-done, bf16[2048,1280]{1,0:T(8,128)(2,1)S(1)} %collective-permute-done.7.other, ...), custom_call_target="tpu_custom_call" | custom-call | flops 2684354560 | bytes 11534336 | tf_op jit(solution)/shard_map/pallas_call | solution.py:229
  36.7 18.5 %all_to_all.11 = f32[128,1,128]{2,1,0:T(1,128)S(1)} all-to-all(f32[128,1,128]{2,1,0:T(1,128)S(1)} %bitcast.10), channel_id=1, replica_groups=mesh['utt'=8,'clu'=16] {'utt','clu'}, dimensions={0} | all-to-all | bytes 131072 | tf_op jit(solution)/shard_map/all_to_all | solution.py:287
  55.2 0.7 %merge.1 = (s32[16,128]{1,0:T(8,128)}, f32[16,128]{1,0:T(8,128)}) custom-call(f32[128,128]{1,0:T(8,128)S(1)} %bitcast.11), custom_call_target="tpu_custom_call" | custom-call | tf_op jit(solution)/shard_map/merge/pallas_call | solution.py:288
  (13 shorter events, 0.1 us)
Async XLA Ops:
  0.6 16.8 %copy-start = (bf16[2048,1280]{1,0:T(8,128)(2,1)S(1)}, bf16[2048,1280]{1,0:T(8,128)(2,1)}, u32[]{:S(2)}) copy-start(bf16[2048,1280]{1,0:T(8,128)(2,1)} %own.7) | copy-start | bytes 15728644
  0.6 14.9 %copy-start.1 = (s32[1,128]{1,0:T(1,128)S(1)}, s32[1,128]{1,0:T(1,128)}, u32[]{:S(2)}) copy-start(s32[1,128]{1,0:T(1,128)} %route.1) | copy-start | bytes 1540
  0.6 22.4 %collective-permute-start.7 = (bf16[2048,1280]{1,0:T(8,128)(2,1)}, bf16[2048,1280]{1,0:T(8,128)(2,1)S(1)}, u32[]{:S(2)}, u32[]{:S(2)}) collective-permute-start(bf16[2048,1280]{1,0:T(8,128)(2,1)} %own.7), channel_id=1, source_target_pairs={{0,16},{4,20},{8,24},{12,28},{1,17},{5,21},{9,25},{13,29},{2,18},{... | collective-permute-start | bytes 15728648 | tf_op jit(solution)/shard_map/ppermute | solution.py:252
  3.1 8.0 %collective-permute-start.3 = (bf16[64,1280]{1,0:T(8,128)(2,1)S(1)}, bf16[64,1280]{1,0:T(8,128)(2,1)S(1)}, u32[]{:S(2)}, u32[]{:S(2)}) collective-permute-start(bf16[64,1280]{1,0:T(8,128)(2,1)S(1)} %cut.1), channel_id=1, source_target_pairs={{0,3},{4,7},{8,11},{12,15},{1,0},{5,4},{9,8},{13,12},{2,1},{6,5},{... | collective-permute-start | bytes 491528 | tf_op jit(solution)/shard_map/ppermute | solution.py:252
  7.1 5.8 %collective-permute-start.4 = (bf16[64,1280]{1,0:T(8,128)(2,1)S(1)}, bf16[64,1280]{1,0:T(8,128)(2,1)S(1)}, u32[]{:S(2)}, u32[]{:S(2)}) collective-permute-start(bf16[64,1280]{1,0:T(8,128)(2,1)S(1)} %cut.1), channel_id=1, source_target_pairs={{0,2},{4,6},{8,10},{12,14},{1,3},{5,7},{9,11},{13,15},{2,0},{6,4},... | collective-permute-start | bytes 491528 | tf_op jit(solution)/shard_map/ppermute | solution.py:252
  7.1 8.3 %collective-permute-start = (bf16[64,1280]{1,0:T(8,128)(2,1)S(1)}, bf16[64,1280]{1,0:T(8,128)(2,1)S(1)}, u32[]{:S(2)}, u32[]{:S(2)}) collective-permute-start(bf16[64,1280]{1,0:T(8,128)(2,1)S(1)} %cut.1), channel_id=1, source_target_pairs={{0,1},{4,5},{8,9},{12,13},{1,2},{5,6},{9,10},{13,14},{2,3},{6,7},{... | collective-permute-start | bytes 491528 | tf_op jit(solution)/shard_map/ppermute | solution.py:252
  12.9 6.6 %collective-permute-start.5 = (bf16[128,1280]{1,0:T(8,128)(2,1)S(1)}, bf16[128,1280]{1,0:T(8,128)(2,1)S(1)}, u32[]{:S(2)}, u32[]{:S(2)}) collective-permute-start(bf16[128,1280]{1,0:T(8,128)(2,1)S(1)} %constant_dynamic-update-slice_fusion.second), channel_id=1, source_target_pairs={{0,12},{4,0},{8,4},{12,8},{1,13},{5,1},{9,5},{13,9},{2,14},{6,2},{... | collective-permute-start | bytes 983048 | tf_op jit(solution)/shard_map/ppermute | solution.py:252
  15.5 7.5 %collective-permute-start.1 = (bf16[128,1280]{1,0:T(8,128)(2,1)S(1)}, bf16[128,1280]{1,0:T(8,128)(2,1)S(1)}, u32[]{:S(2)}, u32[]{:S(2)}) collective-permute-start(bf16[128,1280]{1,0:T(8,128)(2,1)S(1)} %pad_maximum_fusion.first), channel_id=1, source_target_pairs={{0,4},{4,8},{8,12},{12,0},{1,5},{5,9},{9,13},{13,1},{2,6},{6,10},{... | collective-permute-start | bytes 983048 | tf_op jit(solution)/shard_map/ppermute | solution.py:252
  15.6 17.7 %collective-permute-start.10 = (s32[1,128]{1,0:T(1,128)S(1)}, s32[1,128]{1,0:T(1,128)S(1)}, u32[]{:S(2)}, u32[]{:S(2)}) collective-permute-start(s32[1,128]{1,0:T(1,128)S(1)} %copy-done.1), channel_id=1, source_target_pairs={{0,16},{4,20},{8,24},{12,28},{1,17},{5,21},{9,25},{13,29},{2,18},{... | collective-permute-start | bytes 1544 | tf_op jit(solution)/shard_map/ppermute | solution.py:252
  19.0 11.4 %collective-permute-start.9 = (bf16[128,1280]{1,0:T(8,128)(2,1)S(1)}, bf16[128,1280]{1,0:T(8,128)(2,1)S(1)}, u32[]{:S(2)}, u32[]{:S(2)}) collective-permute-start(bf16[128,1280]{1,0:T(8,128)(2,1)S(1)} %constant_dynamic-update-slice_fusion.second), channel_id=1, source_target_pairs={{0,4},{4,8},{8,12},{12,0},{1,5},{5,9},{9,13},{13,1},{2,6},{6,10},{... | collective-permute-start | bytes 983048 | tf_op jit(solution)/shard_map/ppermute | solution.py:252
  19.5 10.9 %collective-permute-start.8 = (bf16[128,1280]{1,0:T(8,128)(2,1)S(1)}, bf16[128,1280]{1,0:T(8,128)(2,1)S(1)}, u32[]{:S(2)}, u32[]{:S(2)}) collective-permute-start(bf16[128,1280]{1,0:T(8,128)(2,1)S(1)} %pad_maximum_fusion.first), channel_id=1, source_target_pairs={{0,12},{4,0},{8,4},{12,8},{1,13},{5,1},{9,5},{13,9},{2,14},{6,2},{... | collective-permute-start | bytes 983048 | tf_op jit(solution)/shard_map/ppermute | solution.py:252
  23.0 10.4 %collective-permute-start.6 = (bf16[128,1280]{1,0:T(8,128)(2,1)S(1)}, bf16[128,1280]{1,0:T(8,128)(2,1)S(1)}, u32[]{:S(2)}, u32[]{:S(2)}) collective-permute-start(bf16[128,1280]{1,0:T(8,128)(2,1)S(1)} %collective-permute-done.5.second), channel_id=1, source_target_pairs={{0,12},{4,0},{8,4},{12,8},{1,13},{5,1},{9,5},{13,9},{2,14},{6,2},{... | collective-permute-start | bytes 983048 | tf_op jit(solution)/shard_map/ppermute | solution.py:252
  23.1 10.3 %collective-permute-start.2 = (bf16[128,1280]{1,0:T(8,128)(2,1)S(1)}, bf16[128,1280]{1,0:T(8,128)(2,1)S(1)}, u32[]{:S(2)}, u32[]{:S(2)}) collective-permute-start(bf16[128,1280]{1,0:T(8,128)(2,1)S(1)} %collective-permute-done.1.first), channel_id=1, source_target_pairs={{0,4},{4,8},{8,12},{12,0},{1,5},{5,9},{9,13},{13,1},{2,6},{6,10},{... | collective-permute-start | bytes 983048 | tf_op jit(solution)/shard_map/ppermute | solution.py:252

commit v2 on v1

--- a/solution.py
+++ b/solution.py
@@ -89,7 +89,7 @@
     )(pltpu.with_memory_space_constraint(centroids, pltpu.HBM))
 
 
-def square_kernel(feat_ref, sq_ref):
+def square_kernel(feat_ref, route_ref, out_ref, sq_ref):
     frames, width = feat_ref.shape
     cell = 256
     eye = (
@@ -103,19 +103,7 @@
             )
             total = total + jnp.sum((part * part).reshape(cell // 8, 8, cell), axis=0)
         sq_ref[:, f : f + cell] = jnp.broadcast_to(jnp.sum(total, axis=0, keepdims=True), (8, cell))
-
-
-def squares(features):
-    frames, _ = features.shape
-    return pl.pallas_call(
-        square_kernel,
-        out_shape=jax.ShapeDtypeStruct((8, frames), F32),
-        in_specs=[pl.BlockSpec(memory_space=VMEM)],
-        out_specs=pl.BlockSpec(memory_space=VMEM),
-        compiler_params=pltpu.CompilerParams(vmem_limit_bytes=2 << 20),
-        cost_estimate=pl.CostEstimate(flops=1 << 30, bytes_accessed=5 << 20, transcendentals=0),
-        name="squares",
-    )(features)
+    out_ref[...] = exact_dot(by_route(route_ref), put(sq_ref[0:1, :], 4))
 
 
 def score(cents, bases, own_ref, other_ref, least_in, index_in, least_ref, index_ref):
@@ -157,48 +145,64 @@
             index_ref[:, at] = index
 
 
-def pieces(value):
-    high = value.astype(BF16)
-    rest = value - high.astype(F32)
-    middle = rest.astype(BF16)
-    low = (rest - middle.astype(F32)).astype(BF16)
-    return high, middle, low
-
-
-def exact_dot(left, right):
+def pieces(value, count):
+    parts = []
+    for _ in range(count):
+        part = value.astype(BF16)
+        parts.append(part)
+        value = value - part.astype(F32)
+    return parts
+
+
+def exact_dot(left, right, count=3):
     if left.dtype == F32:
-        parts = [jnp.dot(p, right, preferred_element_type=F32) for p in pieces(left)]
+        parts = [jnp.dot(p, right, preferred_element_type=F32) for p in pieces(left, count)]
     else:
-        parts = [jnp.dot(left, p, preferred_element_type=F32) for p in pieces(right)]
-    return (parts[0] + parts[1]) + parts[2]
-
-
-def pack(least, index, square_ref, route_ref, other_route_ref, out_ref):
-    frames = least.shape[1] // 2
-    low = jnp.min(least, axis=0, keepdims=True)
-    label = jnp.min(jnp.where(least == low, index, BIG), axis=0, keepdims=True).astype(F32)
-    square = square_ref[0:1, :]
+        parts = [jnp.dot(left, p, preferred_element_type=F32) for p in pieces(right, count)]
+    return sum(parts[1:], parts[0])
+
+
+def put(row, slot, count=3):
     sub = lax.broadcasted_iota(jnp.int32, (8, 128), 0)
     lane = lax.broadcasted_iota(jnp.int32, (8, 128), 1)
     mask = (lane // 16) == sub
     src = lax.broadcasted_iota(jnp.int32, (128, 128), 0)
     dst = lax.broadcasted_iota(jnp.int32, (128, 128), 1)
-
-    def spread(row):
-        groups = [
-            jnp.where(mask, jnp.broadcast_to(row[:, i : i + 128], (8, 128)), 0.0) for i in range(0, frames, 128)
-        ]
-        return jnp.concatenate(groups, axis=0)
-
-    def place(row, slot):
-        pick = (dst == slot * 16 + lax.rem(src, 16)).astype(BF16)
-        return exact_dot(spread(row), pick)
-
-    own = place(low[:, :frames], 0) + place(label[:, :frames], 1) + place(square, 4)
-    other = place(low[:, frames:], 2) + place(label[:, frames:], 3)
-    to_own = (src == route_ref[0:1, :]).astype(BF16)
-    to_other = (src == other_route_ref[0:1, :]).astype(BF16)
-    out_ref[...] = exact_dot(to_own, own) + exact_dot(to_other, other)
+    groups = [
+        jnp.where(mask, jnp.broadcast_to(row[:, i : i + 128], (8, 128)), 0.0) for i in range(0, row.shape[1], 128)
+    ]
+    pick = (dst == slot * 16 + lax.rem(src, 16)).astype(BF16)
+    return exact_dot(jnp.concatenate(groups, axis=0), pick, count)
+
+
+def by_route(route_ref):
+    trainer = lax.broadcasted_iota(jnp.int32, (128, 128), 0)
+    return (trainer == route_ref[0:1, :]).astype(BF16)
+
+
+def pack(least, index, square_ref, route_ref, other_route_ref, out_ref):
+    frames = least.shape[1] // 2
+    low = jnp.min(least, axis=0, keepdims=True)
+    label = jnp.min(jnp.where(least == low, index, BIG), axis=0, keepdims=True).astype(F32)
+    own = put(low[:, :frames], 0) + put(label[:, :frames], 1, 2)
+    other = put(low[:, frames:], 2) + put(label[:, frames:], 3, 2)
+    out_ref[...] = (
+        exact_dot(by_route(route_ref), own) + exact_dot(by_route(other_route_ref), other) + square_ref[...]
+    )
+
+
+def squares(features, route):
+    frames = features.shape[0]
+    return pl.pallas_call(
+        square_kernel,
+        out_shape=jax.ShapeDtypeStruct((128, 128), F32),
+        in_specs=[pl.BlockSpec(memory_space=VMEM)] * 2,
+        out_specs=pl.BlockSpec(memory_space=VMEM),
+        scratch_shapes=[pltpu.VMEM((8, frames), F32)],
+        compiler_params=pltpu.CompilerParams(vmem_limit_bytes=2 << 20),
+        cost_estimate=pl.CostEstimate(flops=1 << 30, bytes_accessed=5 << 20, transcendentals=0),
+        name="squares",
+    )(features, route)
 
 
 def halves(first, first_from, second, second_from):
@@ -269,7 +273,7 @@
     over_first = send(up_first, far_step(1))
     over_second = send(down_second, far_step(-1))
     own = pltpu.with_memory_space_constraint(features, VMEM)
-    square = squares(own)
+    square = squares(own, route)
     state = (jax.ShapeDtypeStruct((8, 2 * frames), F32), jax.ShapeDtypeStruct((8, 2 * frames), jnp.int32))
     least, index = scoring(first_kernel, (first, second, own, other), state)
     least, index = scoring(

time: 56.1 us -> 56.1 us (level)
  transfers between devices with their start and end apart: 11 -> 11, of which waited for: 4 -> 4; matrix products, arithmetic and copies ran while one was open for 0% -> 0% of each run, Pallas kernels for 20% -> 21%
where the time goes in v2:
time: 56.1 us; the launch traced here: 55.9 us
  blocking collectives  18.5 us (33%)
  Pallas kernels  15.8 us (28%)
  starting transfers between devices  15.6 us (28%)
  waiting for transfers between devices  5.24 us (9%)
  between operations  0.77 us (1%)
    all_to_all x1, blocking collectives, labelled(): got = lax.all_to_all(packed, AXES, split_axis=0, concat_axis=0, tiled=True)  18.5 us
    ppermute x11, starting transfers between devices, send(): return lax.ppermute(value, AXES, pairs)  15.6 us
    pallas_call x4, Pallas kernels, scoring(): pl.pallas_call(kernel, out_shape=out_shape, in_specs=[pl.BlockSpec(memory...  12.2 us
    ppermute x11, waiting for transfers between devices, send(): return lax.ppermute(value, AXES, pairs)  5.24 us
    pallas_call x1, Pallas kernels, squares(): pl.pallas_call(square_kernel, out_shape=jax.ShapeDtypeStruct((128, 128),...  1.91 us
  transfers between devices with their start and end apart: 11, of which 4 were waited for; matrix products, arithmetic and copies ran while one was open for 0% of the time, Pallas kernels for 21%

profile of v2, /device:TPU:1, one launch (start us, length us, event | category | flops | bytes accessed | tf_op | source)
XLA Modules:
  0.0 55.9 jit_solution(8090594922498624600)
XLA Ops:
  0.6 1.5 %collective-permute-start.7 = (bf16[2048,1280]{1,0:T(8,128)(2,1)}, bf16[2048,1280]{1,0:T(8,128)(2,1)S(1)}, u32[]{:S(2)}, u32[]{:S(2)}) collective-permute-start(bf16[2048,1280]{1,0:T(8,128)(2,1)} %own.7), channel_id=1, source_target_pairs={{0,16},{4,20},{8,24},{12,28},{1,17},{5,21},{9,25},{13,29},{2,18},{... | collective-permute-start | bytes 15728648 | tf_op jit(solution)/shard_map/ppermute | solution.py:256
  2.1 1.0 %cut.1 = bf16[64,1280]{1,0:T(8,128)(2,1)S(1)} custom-call(bf16[128,1280]{1,0:T(8,128)(2,1)} %cents_hbm.1), custom_call_target="tpu_custom_call" | custom-call | flops 17179869184 | bytes 1048576 | tf_op jit(solution)/shard_map/cut/pallas_call | solution.py:80
  3.1 4.0 %collective-permute-start.3 = (bf16[64,1280]{1,0:T(8,128)(2,1)S(1)}, bf16[64,1280]{1,0:T(8,128)(2,1)S(1)}, u32[]{:S(2)}, u32[]{:S(2)}) collective-permute-start(bf16[64,1280]{1,0:T(8,128)(2,1)S(1)} %cut.1), channel_id=1, source_target_pairs={{0,3},{4,7},{8,11},{12,15},{1,0},{5,4},{9,8},{13,12},{2,1},{6,5},{... | collective-permute-start | bytes 491528 | tf_op jit(solution)/shard_map/ppermute | solution.py:256
  7.1 0.0 collective-permute-start.4
  7.1 0.7 %collective-permute-start = (bf16[64,1280]{1,0:T(8,128)(2,1)S(1)}, bf16[64,1280]{1,0:T(8,128)(2,1)S(1)}, u32[]{:S(2)}, u32[]{:S(2)}) collective-permute-start(bf16[64,1280]{1,0:T(8,128)(2,1)S(1)} %cut.1), channel_id=1, source_target_pairs={{0,1},{4,5},{8,9},{12,13},{1,2},{5,6},{9,10},{13,14},{2,3},{6,7},{... | collective-permute-start | bytes 491528 | tf_op jit(solution)/shard_map/ppermute | solution.py:256
  7.8 3.3 %collective-permute-done.3 = bf16[64,1280]{1,0:T(8,128)(2,1)S(1)} collective-permute-done((bf16[64,1280]{1,0:T(8,128)(2,1)S(1)}, bf16[64,1280]{1,0:T(8,128)(2,1)S(1)}, u32[]{:S(2)}, u32[]{:S(2)}) %collective-permute-start.3) | collective-permute-done | bytes 163872 | tf_op jit(solution)/shard_map/ppermute | solution.py:256
  11.2 1.7 %collective-permute-done.4 = bf16[64,1280]{1,0:T(8,128)(2,1)S(1)} collective-permute-done((bf16[64,1280]{1,0:T(8,128)(2,1)S(1)}, bf16[64,1280]{1,0:T(8,128)(2,1)S(1)}, u32[]{:S(2)}, u32[]{:S(2)}) %collective-permute-start.4) | collective-permute-done | bytes 163872 | tf_op jit(solution)/shard_map/ppermute | solution.py:256
  12.9 2.5 %collective-permute-start.5 = (bf16[128,1280]{1,0:T(8,128)(2,1)S(1)}, bf16[128,1280]{1,0:T(8,128)(2,1)S(1)}, u32[]{:S(2)}, u32[]{:S(2)}) collective-permute-start(bf16[128,1280]{1,0:T(8,128)(2,1)S(1)} %constant_dynamic-update-slice_fusion.second), channel_id=1, source_target_pairs={{0,12},{4,0},{8,4},{12,8},{1,13},{5,1},{9,5},{13,9},{2,14},{6,2},{... | collective-permute-start | bytes 983048 | tf_op jit(solution)/shard_map/ppermute | solution.py:256
  15.5 0.1 collective-permute-start.1
  15.6 1.8 %collective-permute-start.10 = (s32[1,128]{1,0:T(1,128)S(1)}, s32[1,128]{1,0:T(1,128)S(1)}, u32[]{:S(2)}, u32[]{:S(2)}) collective-permute-start(s32[1,128]{1,0:T(1,128)S(1)} %copy-done.1), channel_id=1, source_target_pairs={{0,16},{4,20},{8,24},{12,28},{1,17},{5,21},{9,25},{13,29},{2,18},{... | collective-permute-start | bytes 1544 | tf_op jit(solution)/shard_map/ppermute | solution.py:256
  17.4 1.9 %squares.1.square = f32[128,128]{1,0:T(8,128)S(1)} custom-call(bf16[2048,1280]{1,0:T(8,128)(2,1)S(1)} %copy-done, s32[1,128]{1,0:T(1,128)S(1)} %copy-done.1), custom_call_target="tpu_custom_call" | custom-call | flops 1073741824 | bytes 5242880 | tf_op jit(solution)/shard_map/squares/pallas_call | solution.py:196
  19.3 0.1 collective-permute-start.9
  19.4 0.1 collective-permute-done.5.second
  19.5 3.4 %collective-permute-start.8 = (bf16[128,1280]{1,0:T(8,128)(2,1)S(1)}, bf16[128,1280]{1,0:T(8,128)(2,1)S(1)}, u32[]{:S(2)}, u32[]{:S(2)}) collective-permute-start(bf16[128,1280]{1,0:T(8,128)(2,1)S(1)} %pad_maximum_fusion.first), channel_id=1, source_target_pairs={{0,12},{4,0},{8,4},{12,8},{1,13},{5,1},{9,5},{13,9},{2,14},{6,2},{... | collective-permute-start | bytes 983048 | tf_op jit(solution)/shard_map/ppermute | solution.py:256
  22.9 0.1 collective-permute-done.1.first
  23.0 0.1 collective-permute-start.6
  23.1 0.0 collective-permute-done.7.other
  23.1 1.4 %collective-permute-start.2 = (bf16[128,1280]{1,0:T(8,128)(2,1)S(1)}, bf16[128,1280]{1,0:T(8,128)(2,1)S(1)}, u32[]{:S(2)}, u32[]{:S(2)}) collective-permute-start(bf16[128,1280]{1,0:T(8,128)(2,1)S(1)} %collective-permute-done.1.first), channel_id=1, source_target_pairs={{0,4},{4,8},{8,12},{12,0},{1,5},{5,9},{9,13},{13,1},{2,6},{6,10},{... | collective-permute-start | bytes 983048 | tf_op jit(solution)/shard_map/ppermute | solution.py:256
  24.5 2.9 %shard_map.50 = (f32[8,4096]{1,0:T(8,128)S(1)}, s32[8,4096]{1,0:T(8,128)S(1)}) custom-call(bf16[128,1280]{1,0:T(8,128)(2,1)S(1)} %pad_maximum_fusion.first, bf16[128,1280]{1,0:T(8,128)(2,1)S(1)} %constant_dynamic-update-slice_fusion.second, bf16[2048,1280]{1,0:T(8,128)(2,1)S(1)} %copy-done, bf16[2048,1280]{1,0:T(8,128)(2,1)S(1)} %collective-permute-done.7.other), custom_call_target="tpu_custom_call" | custom-call | flops 2684354560 | bytes 11534336 | tf_op jit(solution)/shard_map/pallas_call | solution.py:233
  27.4 2.9 %shard_map.51 = (f32[8,4096]{1,0:T(8,128)S(1)}, s32[8,4096]{1,0:T(8,128)S(1)}) custom-call(bf16[128,1280]{1,0:T(8,128)(2,1)S(1)} %collective-permute-done.1.first, bf16[128,1280]{1,0:T(8,128)(2,1)S(1)} %collective-permute-done.5.second, bf16[2048,1280]{1,0:T(8,128)(2,1)S(1)} %copy-done, bf16[2048,1280]{1,0:T(8,128)(2,1)S(1)} %collective-permute-done.7.other, ...), custom_call_target="tpu_custom_call" | custom-call | flops 2684354560 | bytes 11534336 | tf_op jit(solution)/shard_map/pallas_call | solution.py:233
  30.4 2.9 %shard_map.52 = (f32[8,4096]{1,0:T(8,128)S(1)}, s32[8,4096]{1,0:T(8,128)S(1)}) custom-call(bf16[128,1280]{1,0:T(8,128)(2,1)S(1)} %collective-permute-done.8.first, bf16[128,1280]{1,0:T(8,128)(2,1)S(1)} %collective-permute-done.9.second, bf16[2048,1280]{1,0:T(8,128)(2,1)S(1)} %copy-done, bf16[2048,1280]{1,0:T(8,128)(2,1)S(1)} %collective-permute-done.7.other, ...), custom_call_target="tpu_custom_call" | custom-call | flops 2684354560 | bytes 11534336 | tf_op jit(solution)/shard_map/pallas_call | solution.py:233
  33.4 3.4 %shard_map.53 = f32[128,128]{1,0:T(8,128)S(1)} custom-call(bf16[128,1280]{1,0:T(8,128)(2,1)S(1)} %collective-permute-done.2.first, bf16[128,1280]{1,0:T(8,128)(2,1)S(1)} %collective-permute-done.6.second, bf16[2048,1280]{1,0:T(8,128)(2,1)S(1)} %copy-done, bf16[2048,1280]{1,0:T(8,128)(2,1)S(1)} %collective-permute-done.7.other, ...), custom_call_target="tpu_custom_call" | custom-call | flops 2684354560 | bytes 11534336 | tf_op jit(solution)/shard_map/pallas_call | solution.py:233
  36.7 18.5 %all_to_all.11 = f32[128,1,128]{2,1,0:T(1,128)S(1)} all-to-all(f32[128,1,128]{2,1,0:T(1,128)S(1)} %bitcast.10), channel_id=1, replica_groups=mesh['utt'=8,'clu'=16] {'utt','clu'}, dimensions={0} | all-to-all | bytes 131072 | tf_op jit(solution)/shard_map/all_to_all | solution.py:291
  55.3 0.7 %merge.1 = (s32[16,128]{1,0:T(8,128)}, f32[16,128]{1,0:T(8,128)}) custom-call(f32[128,128]{1,0:T(8,128)S(1)} %bitcast.11), custom_call_target="tpu_custom_call" | custom-call | tf_op jit(solution)/shard_map/merge/pallas_call | solution.py:292
  (13 shorter events, 0.1 us)
Async XLA Ops:
  0.6 16.8 %copy-start = (bf16[2048,1280]{1,0:T(8,128)(2,1)S(1)}, bf16[2048,1280]{1,0:T(8,128)(2,1)}, u32[]{:S(2)}) copy-start(bf16[2048,1280]{1,0:T(8,128)(2,1)} %own.7) | copy-start | bytes 15728644
  0.6 14.9 %copy-start.1 = (s32[1,128]{1,0:T(1,128)S(1)}, s32[1,128]{1,0:T(1,128)}, u32[]{:S(2)}) copy-start(s32[1,128]{1,0:T(1,128)} %route.1) | copy-start | bytes 1540
  0.6 22.4 %collective-permute-start.7 = (bf16[2048,1280]{1,0:T(8,128)(2,1)}, bf16[2048,1280]{1,0:T(8,128)(2,1)S(1)}, u32[]{:S(2)}, u32[]{:S(2)}) collective-permute-start(bf16[2048,1280]{1,0:T(8,128)(2,1)} %own.7), channel_id=1, source_target_pairs={{0,16},{4,20},{8,24},{12,28},{1,17},{5,21},{9,25},{13,29},{2,18},{... | collective-permute-start | bytes 15728648 | tf_op jit(solution)/shard_map/ppermute | solution.py:256
  3.1 8.0 %collective-permute-start.3 = (bf16[64,1280]{1,0:T(8,128)(2,1)S(1)}, bf16[64,1280]{1,0:T(8,128)(2,1)S(1)}, u32[]{:S(2)}, u32[]{:S(2)}) collective-permute-start(bf16[64,1280]{1,0:T(8,128)(2,1)S(1)} %cut.1), channel_id=1, source_target_pairs={{0,3},{4,7},{8,11},{12,15},{1,0},{5,4},{9,8},{13,12},{2,1},{6,5},{... | collective-permute-start | bytes 491528 | tf_op jit(solution)/shard_map/ppermute | solution.py:256
  7.1 5.8 %collective-permute-start.4 = (bf16[64,1280]{1,0:T(8,128)(2,1)S(1)}, bf16[64,1280]{1,0:T(8,128)(2,1)S(1)}, u32[]{:S(2)}, u32[]{:S(2)}) collective-permute-start(bf16[64,1280]{1,0:T(8,128)(2,1)S(1)} %cut.1), channel_id=1, source_target_pairs={{0,2},{4,6},{8,10},{12,14},{1,3},{5,7},{9,11},{13,15},{2,0},{6,4},... | collective-permute-start | bytes 491528 | tf_op jit(solution)/shard_map/ppermute | solution.py:256
  7.1 8.3 %collective-permute-start = (bf16[64,1280]{1,0:T(8,128)(2,1)S(1)}, bf16[64,1280]{1,0:T(8,128)(2,1)S(1)}, u32[]{:S(2)}, u32[]{:S(2)}) collective-permute-start(bf16[64,1280]{1,0:T(8,128)(2,1)S(1)} %cut.1), channel_id=1, source_target_pairs={{0,1},{4,5},{8,9},{12,13},{1,2},{5,6},{9,10},{13,14},{2,3},{6,7},{... | collective-permute-start | bytes 491528 | tf_op jit(solution)/shard_map/ppermute | solution.py:256
  12.9 6.6 %collective-permute-start.5 = (bf16[128,1280]{1,0:T(8,128)(2,1)S(1)}, bf16[128,1280]{1,0:T(8,128)(2,1)S(1)}, u32[]{:S(2)}, u32[]{:S(2)}) collective-permute-start(bf16[128,1280]{1,0:T(8,128)(2,1)S(1)} %constant_dynamic-update-slice_fusion.second), channel_id=1, source_target_pairs={{0,12},{4,0},{8,4},{12,8},{1,13},{5,1},{9,5},{13,9},{2,14},{6,2},{... | collective-permute-start | bytes 983048 | tf_op jit(solution)/shard_map/ppermute | solution.py:256
  15.5 7.5 %collective-permute-start.1 = (bf16[128,1280]{1,0:T(8,128)(2,1)S(1)}, bf16[128,1280]{1,0:T(8,128)(2,1)S(1)}, u32[]{:S(2)}, u32[]{:S(2)}) collective-permute-start(bf16[128,1280]{1,0:T(8,128)(2,1)S(1)} %pad_maximum_fusion.first), channel_id=1, source_target_pairs={{0,4},{4,8},{8,12},{12,0},{1,5},{5,9},{9,13},{13,1},{2,6},{6,10},{... | collective-permute-start | bytes 983048 | tf_op jit(solution)/shard_map/ppermute | solution.py:256
  15.6 17.7 %collective-permute-start.10 = (s32[1,128]{1,0:T(1,128)S(1)}, s32[1,128]{1,0:T(1,128)S(1)}, u32[]{:S(2)}, u32[]{:S(2)}) collective-permute-start(s32[1,128]{1,0:T(1,128)S(1)} %copy-done.1), channel_id=1, source_target_pairs={{0,16},{4,20},{8,24},{12,28},{1,17},{5,21},{9,25},{13,29},{2,18},{... | collective-permute-start | bytes 1544 | tf_op jit(solution)/shard_map/ppermute | solution.py:256
  19.3 11.0 %collective-permute-start.9 = (bf16[128,1280]{1,0:T(8,128)(2,1)S(1)}, bf16[128,1280]{1,0:T(8,128)(2,1)S(1)}, u32[]{:S(2)}, u32[]{:S(2)}) collective-permute-start(bf16[128,1280]{1,0:T(8,128)(2,1)S(1)} %constant_dynamic-update-slice_fusion.second), channel_id=1, source_target_pairs={{0,4},{4,8},{8,12},{12,0},{1,5},{5,9},{9,13},{13,1},{2,6},{6,10},{... | collective-permute-start | bytes 983048 | tf_op jit(solution)/shard_map/ppermute | solution.py:256
  19.5 10.9 %collective-permute-start.8 = (bf16[128,1280]{1,0:T(8,128)(2,1)S(1)}, bf16[128,1280]{1,0:T(8,128)(2,1)S(1)}, u32[]{:S(2)}, u32[]{:S(2)}) collective-permute-start(bf16[128,1280]{1,0:T(8,128)(2,1)S(1)} %pad_maximum_fusion.first), channel_id=1, source_target_pairs={{0,12},{4,0},{8,4},{12,8},{1,13},{5,1},{9,5},{13,9},{2,14},{6,2},{... | collective-permute-start | bytes 983048 | tf_op jit(solution)/shard_map/ppermute | solution.py:256
  23.0 10.4 %collective-permute-start.6 = (bf16[128,1280]{1,0:T(8,128)(2,1)S(1)}, bf16[128,1280]{1,0:T(8,128)(2,1)S(1)}, u32[]{:S(2)}, u32[]{:S(2)}) collective-permute-start(bf16[128,1280]{1,0:T(8,128)(2,1)S(1)} %collective-permute-done.5.second), channel_id=1, source_target_pairs={{0,12},{4,0},{8,4},{12,8},{1,13},{5,1},{9,5},{13,9},{2,14},{6,2},{... | collective-permute-start | bytes 983048 | tf_op jit(solution)/shard_map/ppermute | solution.py:256
  23.1 10.3 %collective-permute-start.2 = (bf16[128,1280]{1,0:T(8,128)(2,1)S(1)}, bf16[128,1280]{1,0:T(8,128)(2,1)S(1)}, u32[]{:S(2)}, u32[]{:S(2)}) collective-permute-start(bf16[128,1280]{1,0:T(8,128)(2,1)S(1)} %collective-permute-done.1.first), channel_id=1, source_target_pairs={{0,4},{4,8},{8,12},{12,0},{1,5},{5,9},{9,13},{13,1},{2,6},{6,10},{... | collective-permute-start | bytes 983048 | tf_op jit(solution)/shard_map/ppermute | solution.py:256
